TPU v7x, 256 devices: a whole 4x4x8 slice. The times are simulated.
256 devices in a mesh: role: 2 (over z_hi), dp: 16 (over y, z_lo), mp: 8 (over x, core).
Axes of the slice: x: 4, y: 4, z: 8 (z_hi: 2, z_lo: 4; z = z_hi * 4 + z_lo), core: 2. Of those that a mesh axis runs over, the one named last changes fastest.
Arguments:
- patches: bfloat16 [25088, 1280], P('dp', 'mp'), may hold values from -6 to 6
- pred_states: bfloat16 [16384, 384], P('dp'), may hold values from -6 to 6
- ema_up: bfloat16 [1280, 5120], P(('role', 'dp'), 'mp'), may hold values from -0.15625 to 0.15625
- ema_down: bfloat16 [5120, 1280], P('mp', ('role', 'dp')), may hold values from -0.078125 to 0.078125
- pred_up: bfloat16 [384, 1536], P(('role', 'dp'), 'mp'), may hold values from -0.3125 to 0.3125
- pred_down: bfloat16 [1536, 384], P('mp', ('role', 'dp')), may hold values from -0.15625 to 0.15625
- pred_out: bfloat16 [384, 1280], P(('role', 'dp'), 'mp'), may hold values from -0.3125 to 0.3125
- masked_index: int32 [16, 1024], P('dp'), may hold values from 0 to 1567, as said below
- masked_count: int32 [16], P('dp'), may hold values from 512 to 1024, as said below
- loss_scale: float32 [], replicated, may hold values from 81920 to 327680
Outputs:
- loss: float32 [], replicated
- grad_up: float32 [384, 1536], P(('role', 'dp'), 'mp')
- grad_down: float32 [1536, 384], P('mp', ('role', 'dp'))
- grad_out: float32 [384, 1280], P(('role', 'dp'), 'mp')
Inputs may be any that keep to these rules, and one draw needn't show every extreme that they name: `masked_index`: within a clip the slots name distinct tokens; the slots below masked_count name the masked tokens, which are whole tubes: all 8 frames (token f * 196 + s for frame f) of some spatial positions s. Slots from masked_count on name other tokens and are ignored. `masked_count`: each count is 8 times a whole number; some clip has exactly 1024.
All inputs are finite; a program needn't handle non-finite values.
Results may differ from a plain program's by a relative error of at most 0.012.
Values may be sent and summed in bfloat16 or wider, within the bound.
No kernel may reach another device: no remote copies, remote signals or barrier semaphores. Data moves between devices by JAX's collectives and lax.ppermute only.
A program may use at most 128 MiB of HBM per device.

v0:
```python
import functools
import jax
import jax.numpy as jnp
from jax import lax
from jax.sharding import Mesh
from jax.sharding import PartitionSpec as P

D = 1280
TOK = 1568
MMAX = 1024
MP = ("mp_0", "mp_1")
ROLE_DP = ("role", "dp_0", "dp_1")
DP = ("dp_0", "dp_1")
ROLE_DP_MP = ("role", "dp_0", "dp_1", "mp_0", "mp_1")
EPS = 1e-06
COEF = 0.7978845608028654


def joined_along(pieces, dim):
    pieces = jnp.moveaxis(pieces, 0, dim)
    lengths = pieces.shape
    return pieces.reshape(*lengths[:dim], lengths[dim] * lengths[dim + 1], *lengths[dim + 2 :])


def from_everyone(shard, axis):
    copies = jnp.broadcast_to(shard, (lax.axis_size(axis), *shard.shape))
    return lax.all_to_all(copies, axis, split_axis=0, concat_axis=0, tiled=True)


def gather_directly(shard, axis, dim):
    return joined_along(from_everyone(shard, axis), dim)


def of_everyone(shard, axis):
    return from_everyone(shard, axis).sum(axis=0)


def in_one(arrays, axis):
    vector, at, outs = (jnp.concatenate([a.reshape(-1) for a in arrays]), 0, [])
    total = of_everyone(vector, axis)
    for a in arrays:
        outs.append(total[at : at + a.size].reshape(a.shape))
        at += a.size
    return tuple(outs)


def passed_along(block, axis, distance):
    devices = range(lax.axis_size(axis))
    route = [(i - distance, i) for i in devices if i - distance in devices]
    return lax.ppermute(block, axis, route)


def sent_together(arrays, axis, dim, along):
    widths = [a.shape[along] for a in arrays]
    both = jnp.concatenate(arrays, axis=along)
    filled = lax.all_gather(both, axis, axis=dim, tiled=True)
    return tuple(jnp.split(filled, [sum(widths[:k]) for k in range(1, len(widths))], axis=along))


def by_axis(shard, axes):
    return functools.reduce(lax.psum, axes, shard)


def filled_up(lines, devices):
    spare = -len(lines) % devices
    return jnp.pad(lines, [(0, spare)] + [(0, 0)] * (lines.ndim - 1))


def sum_by_parts(shard, axis):
    lines = shard.reshape(-1, *shard.shape[1:][-1:])
    own = lax.psum_scatter(
        filled_up(lines, lax.axis_size(axis)), axis, scatter_dimension=0, tiled=True
    )
    whole = lax.all_gather(own, axis).reshape(-1, *lines.shape[1:])
    return lax.slice_in_dim(whole, 0, len(lines)).reshape(shard.shape)


def cut_along(shard, dim, devices):
    before, after = (shard.shape[:dim], shard.shape[dim + 1 :])
    return jnp.moveaxis(shard.reshape(*before, devices, -1, *after), dim, 0)


def sum_together(arrays, axis, dims):
    devices = lax.axis_size(axis)
    pieces = [cut_along(a, dim, devices) for a, dim in zip(arrays, dims)]
    lines = jnp.concatenate([b.reshape(devices, -1) for b in pieces], axis=1)
    width = max(16, -(-lines.shape[1] // 1024) * 8)
    lines = jnp.pad(lines, ((0, 0), (0, width * 128 - lines.shape[1]))).reshape(-1, 128)
    vector, at, outs = (lax.psum_scatter(lines, axis, tiled=True).reshape(-1), 0, [])
    for b in pieces:
        part = b[0]
        outs.append(vector[at : at + part.size].reshape(part.shape))
        at += part.size
    return tuple(outs)


def summed_on_arrival(shard, axis, dim):
    pieces = cut_along(shard, dim, lax.axis_size(axis))
    arrived = lax.all_to_all(pieces, axis, split_axis=0, concat_axis=0, tiled=True)
    return arrived.sum(axis=0)


def normalize(values):
    row_mean = jnp.mean(values, axis=-1, keepdims=True)
    row_deviations = values - row_mean
    variance = jnp.mean(row_deviations * row_deviations, axis=-1, keepdims=True)
    return row_deviations * lax.rsqrt(variance + EPS)


def gelu_slope(values):
    inner = COEF * (values + 0.044715 * values * values * values)
    tangent = jnp.tanh(inner)
    return 0.5 * (1.0 + tangent) + 0.5 * values * (1.0 - tangent * tangent) * COEF * (
        1.0 + 3.0 * 0.044715 * values * values
    )


def pick_rows(source_table, token_index):
    clip_count = token_index.shape[0]
    slot_total = token_index.shape[1]
    clip_grid = source_table.reshape(clip_count, TOK, source_table.shape[1])
    onehot = (token_index[:, :, None] == jnp.arange(TOK, dtype=jnp.int32)[None, None, :]).astype(
        jnp.bfloat16
    )
    picked = jnp.einsum("ckt,ctw->ckw", onehot, clip_grid, preferred_element_type=jnp.float32)
    return picked.astype(jnp.bfloat16).reshape(clip_count * slot_total, source_table.shape[1])


def body(
    patches,
    pred_states,
    ema_up,
    ema_down,
    pred_up,
    pred_down,
    pred_out,
    masked_index,
    masked_count,
    loss_scale,
):
    role_index = lax.axis_index("role")
    clip_count = masked_index.shape[0]
    feat_width = float(D)
    half_slots = MMAX // 2
    half_index = lax.dynamic_slice_in_dim(masked_index, role_index * half_slots, half_slots, 1)
    own_rows = pick_rows(patches, half_index)
    whole_rows = gather_directly(own_rows, MP, 1)
    working = role_index >= 0
    block_rows = own_rows.shape[0]
    up_cols = lax.all_gather(ema_up, ROLE_DP, axis=0, tiled=True)
    down_rows = lax.all_gather(ema_down, ROLE_DP, axis=1, tiled=True)

    def encode_block():
        normed = normalize(whole_rows.astype(jnp.float32)).astype(jnp.bfloat16)
        hidden = jax.nn.gelu(
            jnp.dot(normed, up_cols, preferred_element_type=jnp.float32), approximate=True
        ).astype(jnp.bfloat16)
        return jnp.dot(hidden, down_rows, preferred_element_type=jnp.float32)

    def skip_block():
        return jnp.zeros((block_rows, whole_rows.shape[1]), jnp.float32)

    partial_sum = lax.cond(working, encode_block, skip_block)
    branch = lax.psum_scatter(partial_sum, MP, scatter_dimension=1, tiled=True)
    block_out = own_rows.astype(jnp.float32) + branch
    first_sum, second_sum = in_one(
        (
            jnp.sum(block_out, axis=-1, keepdims=True),
            jnp.sum(block_out * block_out, axis=-1, keepdims=True),
        ),
        MP,
    )
    row_mean = first_sum / feat_width
    row_deviations = block_out - row_mean
    variance = second_sum / feat_width - row_mean * row_mean
    target_all = (row_deviations * lax.rsqrt(variance + EPS)).astype(jnp.bfloat16)
    local_width = target_all.shape[1]
    earlier = passed_along(target_all, "role", 1)
    joined = jnp.concatenate(
        (
            earlier.reshape(clip_count, half_slots, local_width),
            target_all.reshape(clip_count, half_slots, local_width),
        ),
        axis=1,
    )
    targets = joined.reshape(clip_count * MMAX, local_width)
    up_rows, out_rows = sent_together((pred_up, pred_out), ROLE_DP, 0, 1)
    down_cols = gather_directly(pred_down, ROLE_DP, 1)
    total = of_everyone(jnp.sum(masked_count).astype(jnp.float32), DP)
    states = pred_states.astype(jnp.float32)
    pnormed = normalize(states).astype(jnp.bfloat16)
    preact = jnp.dot(pnormed, up_rows, preferred_element_type=jnp.float32)
    hid_act = jax.nn.gelu(preact, approximate=True).astype(jnp.bfloat16)
    mixer_out = lax.psum(jnp.dot(hid_act, down_cols, preferred_element_type=jnp.float32), MP)
    updated = states + mixer_out
    row_mean_p = jnp.mean(updated, axis=-1, keepdims=True)
    predictor_deviations = updated - row_mean_p
    reciprocal_spread = lax.rsqrt(
        jnp.mean(predictor_deviations * predictor_deviations, axis=-1, keepdims=True) + EPS
    )
    standardized_input = predictor_deviations * reciprocal_spread
    output_normalized = standardized_input.astype(jnp.bfloat16)
    predicted = jnp.dot(output_normalized, out_rows, preferred_element_type=jnp.float32)
    live_mask = (
        (jnp.arange(MMAX, dtype=jnp.int32)[None, :] < masked_count[:, None])
        .astype(jnp.float32)
        .reshape(clip_count * MMAX, 1)
    )
    predictor_side = (role_index == 1).astype(jnp.float32)
    norm_scale = total * feat_width
    residue = predicted - targets.astype(jnp.float32)
    smooth = jnp.sqrt(residue * residue + 1.0)
    local_loss = jnp.sum(live_mask * (smooth - 1.0)) * predictor_side
    loss = by_axis(local_loss, ROLE_DP_MP) / norm_scale
    grad_pred = (loss_scale * live_mask * residue / smooth / norm_scale * predictor_side).astype(
        jnp.bfloat16
    )
    normalized_gradient = sum_by_parts(
        jnp.einsum("rd,kd->rk", grad_pred, out_rows, preferred_element_type=jnp.float32), MP
    )
    gradient_update = reciprocal_spread * (
        normalized_gradient
        - jnp.mean(normalized_gradient, axis=-1, keepdims=True)
        - standardized_input
        * jnp.mean(normalized_gradient * standardized_input, axis=-1, keepdims=True)
    )
    gradient_update = gradient_update.astype(jnp.bfloat16)
    down_local = jnp.einsum(
        "rf,rk->fk", hid_act, gradient_update, preferred_element_type=jnp.float32
    )
    grad_act = jnp.einsum(
        "rk,fk->rf", gradient_update, down_cols, preferred_element_type=jnp.float32
    )
    grad_pre = (grad_act * gelu_slope(preact)).astype(jnp.bfloat16)
    up_local = jnp.einsum("rk,rf->kf", pnormed, grad_pre, preferred_element_type=jnp.float32)
    out_local = jnp.einsum(
        "rk,rd->kd", output_normalized, grad_pred, preferred_element_type=jnp.float32
    )
    grad_up, grad_out = tuple(
        (
            part.astype(jnp.float32)
            for part in sum_together(
                (up_local.astype(jnp.bfloat16), out_local.astype(jnp.bfloat16)), ROLE_DP, (0, 0)
            )
        )
    )
    grad_down = summed_on_arrival(down_local, ROLE_DP, 1)
    return (loss, grad_up, grad_down, grad_out)


def solution(mesh):
    finer = Mesh(
        mesh.devices.reshape(mesh.shape["role"], 4, 4, 4, 2),
        ("role", "dp_0", "dp_1", "mp_0", "mp_1"),
    )
    return jax.shard_map(
        body,
        mesh=finer,
        in_specs=(
            P(DP, MP),
            P(DP, None),
            P(ROLE_DP, MP),
            P(MP, ROLE_DP),
            P(ROLE_DP, MP),
            P(MP, ROLE_DP),
            P(ROLE_DP, MP),
            P(DP, None),
            P(DP),
            P(),
        ),
        out_specs=(P(), P(ROLE_DP, MP), P(MP, ROLE_DP), P(ROLE_DP, MP)),
        check_vma=False,
    )
```

profile of v0, /device:TPU:2, one launch (start us, length us, event | category | flops | bytes accessed | tf_op | source)
XLA Modules:
  0.0 619.0 jit_solution(12182839815354292576)
XLA Ops:
  10.9 11.5 %all-to-all-start = ((bf16[32,192,12]{1,2,0:T(8,128)(2,1)}), bf16[32,192,12]{1,2,0:T(8,128)(2,1)S(1)}, u32[]{:S(2)}, u32[]{:S(2)}) async-start(bf16[32,192,12]{1,2,0:T(8,128)(2,1)} %broadcast_in_dim.10), calls=%async_computation | async-start | bytes 524288 | tf_op jit(solution)/shard_map/all_to_all | solution.py:27
  23.2 75.8 %all-gather.1 = bf16[32,12,352]{2,1,0:T(8,128)(2,1)S(1)} all-gather(bf16[1,12,352]{2,1,0:T(8,128)(2,1)S(1)} %maximum_bitcast_fusion.1), channel_id=1, replica_groups=mesh['role'=2,'dp_0'=4,'dp_1'=4,'mp_0'=4,'mp_1'=2] {'role','dp_0','dp_1'}, dimensions={0}, use_global_device_ids=true | all-gather | bytes 278784 | tf_op jit(solution)/shard_map/all_gather | solution.py:56
  102.9 4.8 all-to-all-start.1
  113.9 11.1 %all-to-all-done.1 = bf16[8,512,160]{1,2,0:T(8,128)(2,1)S(1)} async-done(((bf16[8,512,160]{1,2,0:T(8,128)(2,1)}), bf16[8,512,160]{1,2,0:T(8,128)(2,1)S(1)}, u32[]{:S(2)}, u32[]{:S(2)}) %all-to-all-start.1) | async-done | bytes 1310752 | tf_op jit(solution)/shard_map/all_to_all | solution.py:27
  124.9 32.0 %all-gather.6.cloned.1.call-done = bf16[1280,640]{1,0:T(8,128)(2,1)} async-done(((bf16[40,640]{1,0:T(8,128)(2,1)}), bf16[1280,640]{1,0:T(8,128)(2,1)}) %all-gather.6.cloned.1.call-update) | async-done | bytes 1638416 | tf_op jit(solution)/shard_map/all_gather | solution.py:150
  156.9 142.1 %all-gather.8.cloned.1.call-done = bf16[640,1280]{0,1:T(8,128)(2,1)} async-done(((bf16[640,40]{0,1:T(8,128)(2,1)}), bf16[640,1280]{0,1:T(8,128)(2,1)}) %all-gather.8.cloned.1.call-update) | async-done | bytes 1638416 | tf_op jit(solution)/shard_map/all_gather | solution.py:151
  299.0 8.5 %conditional.1 = (f32[512,1280]{1,0:T(8,128)}) conditional(s32[]{:T(128)} %convert_element_type.101, () %tuple.14, (bf16[512,8,160]{0,2,1:T(8,128)(2,1)S(1)}, bf16[1280,640]{1,0:T(8,128)(2,1)}, bf16[640,1280]{0,1:T(8,128)(2,1)}) %tuple.41), branch_computations={%region_5.0_spmd, %region_6.9_spmd} | conditional | flops 1687224832 | bytes 12470280 | solution.py:163
  301.1 6.4 %fusion.10 = f32[512,1280]{1,0:T(8,128)} fusion(bf16[640,1280]{0,1:T(8,128)(2,1)} %get-tuple-element.25, bf16[512,1280]{0,1:T(8,128)(2,1)} %fusion.1, bf16[1280,640]{1,0:T(8,128)(2,1)} %get-tuple-element.11), kind=kOutput, calls=%fused_computation.14 | convolution fusion | flops 1680670720 | bytes 7208960 | tf_op jit(solution)/shard_map/cond/branch_1_fun/dot_general | solution.py:158
  307.5 3.2 copy.34
  312.0 5.7 all-to-all-start.3
  318.4 7.2 %all-to-all-done.3 = f32[16,1,1]{2,1,0:T(1,128)S(1)} async-done(((f32[16,1,1]{2,1,0:T(1,128)}), f32[16,1,1]{2,1,0:T(1,128)S(1)}, u32[]{:S(2)}, u32[]{:S(2)}) %all-to-all-start.3) | async-done | bytes 96 | tf_op jit(solution)/shard_map/all_to_all | solution.py:27
  329.3 13.2 %reduce-scatter.3.cloned.1.call-done = f32[512,160]{0,1:T(8,128)} async-done(((f32[512,1280]{0,1:T(8,128)}), f32[512,160]{0,1:T(8,128)}) %reduce-scatter.3.cloned.1.call-update) | async-done | bytes 327696 | tf_op jit(solution)/shard_map/reduce_scatter | solution.py:164
  344.2 7.0 %all-to-all-start.2 = ((f32[8,1,1024]{2,1,0:T(1,128)}), f32[8,1,1024]{2,1,0:T(1,128)S(1)}, u32[]{:S(2)}, u32[]{:S(2)}) async-start(f32[8,1,1024]{2,1,0:T(1,128)} %broadcast_in_dim.12), calls=%async_computation.3 | async-start | bytes 65536 | tf_op jit(solution)/shard_map/all_to_all | solution.py:27
  351.2 4.0 all-to-all-done.2
  356.3 7.8 %collective-permute-start = (bf16[512,160]{0,1:T(8,128)(2,1)S(1)}, bf16[512,160]{0,1:T(8,128)(2,1)S(1)}, u32[]{:S(2)}, u32[]{:S(2)}) collective-permute-start(bf16[512,160]{0,1:T(8,128)(2,1)S(1)} %multiply_convert_fusion.2), channel_id=1, source_target_pairs={{0,128},{1,129},{2,130},{3,131},{4,132},{5,133},{6,134},{7,135},{8... | collective-permute-start | bytes 491528 | tf_op jit(solution)/shard_map/ppermute | solution.py:50
  371.0 36.0 %reduce-scatter.5.cloned.1.call-done = f32[128,384]{1,0:T(8,128)} async-done(((f32[1024,384]{1,0:T(8,128)}), f32[128,384]{1,0:T(8,128)}) %reduce-scatter.5.cloned.1.call-update) | async-done | bytes 196624 | tf_op jit(solution)/shard_map/reduce_scatter | solution.py:71
  408.8 27.1 %all-gather.10.cloned.1.call-done = f32[1024,384]{1,0:T(8,128)} async-done(((f32[128,384]{1,0:T(8,128)}), f32[1024,384]{1,0:T(8,128)}) %all-gather.10.cloned.1.call-update) | async-done | bytes 1572880 | tf_op jit(solution)/shard_map/all_gather | solution.py:74
  444.4 10.0 %all-to-all-start.4 = ((f32[32,192,12]{1,2,0:T(8,128)}), f32[32,192,12]{1,2,0:T(8,128)S(1)}, u32[]{:S(2)}, u32[]{:S(2)}) async-start(f32[32,192,12]{1,2,0:T(8,128)} %bitcast.9), calls=%async_computation.6 | async-start | bytes 1048576 | tf_op jit(solution)/shard_map/all_to_all | solution.py:99
  456.4 16.2 %psum.43 = f32[]{:T(128)} all-reduce(f32[]{:T(128)S(6)} %mul.192), channel_id=1, replica_groups=mesh['role'=2,'dp_0'=4,'dp_1'=4,'mp_0'=4,'mp_1'=2] {'role'}, use_global_device_ids=true, to_apply=%region_14.0 | all-reduce | flops 1 | bytes 8 | tf_op jit(solution)/shard_map/psum | solution.py:61
  472.6 10.4 %psum.44 = f32[]{:T(128)} all-reduce(f32[]{:T(128)} %psum.43), channel_id=1, replica_groups=mesh['role'=2,'dp_0'=4,'dp_1'=4,'mp_0'=4,'mp_1'=2] {'dp_0'}, use_global_device_ids=true, to_apply=%region_15.0 | all-reduce | flops 1 | bytes 8 | tf_op jit(solution)/shard_map/psum | solution.py:61
  483.6 10.3 %psum.45 = f32[]{:T(128)} all-reduce(f32[]{:T(128)} %psum.44), channel_id=1, replica_groups=mesh['role'=2,'dp_0'=4,'dp_1'=4,'mp_0'=4,'mp_1'=2] {'dp_1'}, use_global_device_ids=true, to_apply=%region_16.0 | all-reduce | flops 1 | bytes 8 | tf_op jit(solution)/shard_map/psum | solution.py:61
  494.5 10.4 %psum.46 = f32[]{:T(128)} all-reduce(f32[]{:T(128)} %psum.45), channel_id=1, replica_groups=mesh['role'=2,'dp_0'=4,'dp_1'=4,'mp_0'=4,'mp_1'=2] {'mp_0'}, use_global_device_ids=true, to_apply=%region_17.0 | all-reduce | flops 1 | bytes 8 | tf_op jit(solution)/shard_map/psum | solution.py:61
  504.9 3.1 psum.47
  508.6 98.4 %all-reduce.7.cloned.1.call-done = bf16[1280,128]{1,0:T(8,128)(2,1)} async-done(((bf16[1280,128]{1,0:T(8,128)(2,1)}), bf16[1280,128]{1,0:T(8,128)(2,1)}) %all-reduce.7.cloned.1.call-update) | async-done | bytes 327696
  (104 shorter events, 44.5 us)
Async XLA Ops:
  8.0 92.6 %copy-start = (bf16[1568,160]{0,1:T(8,128)(2,1)S(1)}, bf16[1568,160]{0,1:T(8,128)(2,1)}, u32[]{:S(2)}) copy-start(bf16[1568,160]{0,1:T(8,128)(2,1)} %param.12) | copy-start | bytes 1505284
  8.0 91.0 %copy-start.1 = (bf16[1024,384]{1,0:T(8,128)(2,1)S(1)}, bf16[1024,384]{1,0:T(8,128)(2,1)}, u32[]{:S(2)}) copy-start(bf16[1024,384]{1,0:T(8,128)(2,1)} %param.13) | copy-start | bytes 2359300
  8.0 91.7 %copy-start.14 = (s32[1,1024]{1,0:T(1,128)S(1)}, s32[1,1024]{1,0:T(1,128)}, u32[]{:S(2)}) copy-start(s32[1,1024]{1,0:T(1,128)} %param.19) | copy-start | bytes 12292
  8.0 148.9 %all-gather.6.cloned.1.call-start = ((), (), s32[]{:S(2)}) async-start(), calls=%async_computation.8 | async-start | bytes 1689600 | tf_op jit(solution)/shard_map/all_gather | solution.py:150
  8.8 290.2 %all-gather.8.cloned.1.call-start = ((), (), s32[]{:S(2)}) async-start(), calls=%async_computation.9 | async-start | bytes 1689600 | tf_op jit(solution)/shard_map/all_gather | solution.py:151
  10.9 90.7 %all-to-all-start = ((bf16[32,192,12]{1,2,0:T(8,128)(2,1)}), bf16[32,192,12]{1,2,0:T(8,128)(2,1)S(1)}, u32[]{:S(2)}, u32[]{:S(2)}) async-start(bf16[32,192,12]{1,2,0:T(8,128)(2,1)} %broadcast_in_dim.10), calls=%async_computation | async-start | bytes 524288 | tf_op jit(solution)/shard_map/all_to_all | solution.py:27
  102.9 22.0 %all-to-all-start.1 = ((bf16[8,512,160]{1,2,0:T(8,128)(2,1)}), bf16[8,512,160]{1,2,0:T(8,128)(2,1)S(1)}, u32[]{:S(2)}, u32[]{:S(2)}) async-start(bf16[8,512,160]{1,2,0:T(8,128)(2,1)} %broadcast_in_dim.11), calls=%async_computation.1 | async-start | bytes 2621440 | tf_op jit(solution)/shard_map/all_to_all | solution.py:27
  107.7 219.2 %all-reduce.5.cloned.1.call-start = ((), (), s32[]{:S(2)}) async-start(), calls=%async_computation.7 | async-start | bytes 3145728 | tf_op jit(solution)/shard_map/psum | solution.py:194
  109.3 4.5 copy-start.4
  113.8 228.6 %reduce-scatter.3.cloned.1.call-start = ((), (), s32[]{:S(2)}) async-start(), calls=%async_computation.10 | async-start | bytes 2949120 | tf_op jit(solution)/shard_map/reduce_scatter | solution.py:164
  312.0 13.6 %all-to-all-start.3 = ((f32[16,1,1]{2,1,0:T(1,128)}), f32[16,1,1]{2,1,0:T(1,128)S(1)}, u32[]{:S(2)}, u32[]{:S(2)}) async-start(f32[16,1,1]{2,1,0:T(1,128)} %broadcast_in_dim.13), calls=%async_computation.4 | async-start | bytes 16384 | tf_op jit(solution)/shard_map/all_to_all | solution.py:27
  326.8 1.9 copy-start.2
  328.7 13.8 %copy-start.10 = (bf16[512,160]{0,1:T(8,128)(2,1)S(1)}, bf16[512,160]{0,1:T(8,128)(2,1)}, u32[]{:S(2)}) copy-start(bf16[512,160]{0,1:T(8,128)(2,1)} %copy-done.9) | copy-start | bytes 491524
  344.2 11.1 %all-to-all-start.2 = ((f32[8,1,1024]{2,1,0:T(1,128)}), f32[8,1,1024]{2,1,0:T(1,128)S(1)}, u32[]{:S(2)}, u32[]{:S(2)}) async-start(f32[8,1,1024]{2,1,0:T(1,128)} %broadcast_in_dim.12), calls=%async_computation.3 | async-start | bytes 65536 | tf_op jit(solution)/shard_map/all_to_all | solution.py:27
  351.2 55.7 %reduce-scatter.5.cloned.1.call-start = ((), (), s32[]{:S(2)}) async-start(), calls=%async_computation.11 | async-start | bytes 1769472 | tf_op jit(solution)/shard_map/reduce_scatter | solution.py:71
  356.3 11.2 %copy-start.8 = (bf16[384,352]{1,0:T(8,128)(2,1)S(1)}, bf16[384,352]{1,0:T(8,128)(2,1)}, u32[]{:S(2)}) copy-start(bf16[384,352]{1,0:T(8,128)(2,1)} %reshape.189) | copy-start | bytes 811012
  356.3 11.1 %collective-permute-start = (bf16[512,160]{0,1:T(8,128)(2,1)S(1)}, bf16[512,160]{0,1:T(8,128)(2,1)S(1)}, u32[]{:S(2)}, u32[]{:S(2)}) collective-permute-start(bf16[512,160]{0,1:T(8,128)(2,1)S(1)} %multiply_convert_fusion.2), channel_id=1, source_target_pairs={{0,128},{1,129},{2,130},{3,131},{4,132},{5,133},{6,134},{7,135},{8... | collective-permute-start | bytes 491528 | tf_op jit(solution)/shard_map/ppermute | solution.py:50
  364.5 4.5 copy-start.7
  370.7 65.2 %all-gather.10.cloned.1.call-start = ((), (), s32[]{:S(2)}) async-start(), calls=%async_computation.12 | async-start | bytes 1769472 | tf_op jit(solution)/shard_map/all_gather | solution.py:74
  436.0 2.3 copy-start.3
  438.2 1.8 copy-start.5
  444.4 38.6 %copy-start.15 = (u32[256]{0:T(256)S(1)}, u32[256]{0:T(256)}, u32[]{:S(2)}) copy-start(u32[256]{0:T(256)} %constant.79) | copy-start | bytes 3076
  444.4 165.4 %all-to-all-start.4 = ((f32[32,192,12]{1,2,0:T(8,128)}), f32[32,192,12]{1,2,0:T(8,128)S(1)}, u32[]{:S(2)}, u32[]{:S(2)}) async-start(f32[32,192,12]{1,2,0:T(8,128)} %bitcast.9), calls=%async_computation.6 | async-start | bytes 1048576 | tf_op jit(solution)/shard_map/all_to_all | solution.py:99
  454.4 152.7 %all-reduce.7.cloned.1.call-start = ((), (), s32[]{:S(2)}) async-start(), calls=%async_computation.13 | async-start | bytes 655360
  (5 other events, 5.8 us)
Sparse Core Ops, SparseCore 0:
  10.6 146.2 all-gather.5
  158.7 140.2 all-gather.7
  458.6 148.3 all-reduce.6
Sparse Core Ops, SparseCore 1:
  113.9 67.6 all-reduce.4
  310.8 31.6 reduce-scatter.2
  370.8 36.1 reduce-scatter.4
  408.8 27.1 all-gather.9
where the time goes:
time: 620 us; the launch traced here: 619 us
  waiting for transfers between devices  375 us (60%)
  blocking collectives  126 us (20%)
  starting transfers between devices  47.1 us (8%)
  between operations  20.9 us (3%)
  matrix products  19.1 us (3%)
  local copies, waits for them, and re-layouts  15.9 us (3%)
  other arithmetic  14.2 us (2%)
    all_gather x1, waiting for transfers between devices, body(): down_rows = lax.all_gather(ema_down, ROLE_DP, axis=1, tiled=True)  142 us
    unnamed x8, waiting for transfers between devices  99.9 us
    all_gather x1, blocking collectives, sent_together(): filled = lax.all_gather(both, axis, axis=dim, tiled=True)  75.8 us
    psum x5, blocking collectives, by_axis(): return functools.reduce(lax.psum, axes, shard)  50.4 us
    reduce_scatter x1, waiting for transfers between devices, sum_by_parts(): lax.psum_scatter(filled_up(lines, lax.axis_size(axis)), axis, scatter_dim...  36 us
    all_gather x1, waiting for transfers between devices, body(): up_cols = lax.all_gather(ema_up, ROLE_DP, axis=0, tiled=True)  32 us
    all_to_all x4, starting transfers between devices, from_everyone(): return lax.all_to_all(copies, axis, split_axis=0, concat_axis=0, tiled=True)  29 us
    all_gather x1, waiting for transfers between devices, sum_by_parts(): whole = lax.all_gather(own, axis).reshape(-1, *lines.shape[1:])  27.1 us
  transfers between devices with their start and end apart: 13, of which 10 were waited for; matrix products, arithmetic and copies ran while one was open for 6% of the time, Pallas kernels for 0%

commit v1 on v0

--- a/solution.py
+++ b/solution.py
@@ -147,7 +147,8 @@
     whole_rows = gather_directly(own_rows, MP, 1)
     working = role_index >= 0
     block_rows = own_rows.shape[0]
-    up_cols = lax.all_gather(ema_up, ROLE_DP, axis=0, tiled=True)
+    sent = jnp.stack([ema_up] * lax.axis_size(ROLE_DP))
+    up_cols = jnp.concatenate(lax.all_to_all(sent, ROLE_DP, 0, 0), axis=0)
     down_rows = lax.all_gather(ema_down, ROLE_DP, axis=1, tiled=True)
 
     def encode_block():

time: 620 us -> 566 us (0.913)
  waiting for transfers between devices: 375 us -> 280 us
  blocking collectives: 126 us -> 164 us
    all_gather x1, waiting for transfers between devices: 142 us -> 4.71 us  [body(): down_rows = lax.all_gather(ema_down, ROLE_DP, axis=1, tiled=True)]
    all_gather x1, blocking collectives: 75.8 us -> 113 us  [sent_together(): filled = lax.all_gather(both, axis, axis=dim, tiled=True)]
    psum x1, waiting for transfers between devices: 0.03 us -> 34.8 us  [body(): lax.psum(jnp.dot(hid_act, down_cols, preferred_element_type=jnp.float32),...]
    all_gather x1 -> x0, waiting for transfers between devices: 32 us -> none  [body(): up_cols = lax.all_gather(ema_up, ROLE_DP, axis=0, tiled=True)]
    reduce_scatter x1, waiting for transfers between devices: 13.2 us -> 35.9 us  [body(): branch = lax.psum_scatter(partial_sum, MP, scatter_dimension=1, tiled=True)]
    all_to_all x4, waiting for transfers between devices: 22.2 us -> 39.6 us  [from_everyone(): return lax.all_to_all(copies, axis, split_axis=0, concat_axis=0, tiled=True)]
    unnamed x8 -> x7, waiting for transfers between devices: 99.9 us -> 99.2 us
  transfers between devices with their start and end apart: 13 -> 13, of which waited for: 10 -> 11; matrix products, arithmetic and copies ran while one was open for 6% -> 6% of each run, Pallas kernels for 0% -> 0%
where the time goes in v1:
time: 566 us; the launch traced here: 565 us
  waiting for transfers between devices  280 us (49%)
  blocking collectives  164 us (29%)
  starting transfers between devices  50 us (9%)
  between operations  21.1 us (4%)
  local copies, waits for them, and re-layouts  18.2 us (3%)
  matrix products  18.2 us (3%)
  other arithmetic  13.5 us (2%)
    all_gather x1, blocking collectives, sent_together(): filled = lax.all_gather(both, axis, axis=dim, tiled=True)  113 us
    unnamed x7, waiting for transfers between devices  99.2 us
    psum x5, blocking collectives, by_axis(): return functools.reduce(lax.psum, axes, shard)  50.4 us
    all_to_all x4, waiting for transfers between devices, from_everyone(): return lax.all_to_all(copies, axis, split_axis=0, concat_axis=0, tiled=True)  39.6 us
    reduce_scatter x1, waiting for transfers between devices, sum_by_parts(): lax.psum_scatter(filled_up(lines, lax.axis_size(axis)), axis, scatter_dim...  35.9 us
    reduce_scatter x1, waiting for transfers between devices, body(): branch = lax.psum_scatter(partial_sum, MP, scatter_dimension=1, tiled=True)  35.9 us
    psum x1, waiting for transfers between devices, body(): lax.psum(jnp.dot(hid_act, down_cols, preferred_element_type=jnp.float32),...  34.8 us
    all_gather x1, waiting for transfers between devices, sum_by_parts(): whole = lax.all_gather(own, axis).reshape(-1, *lines.shape[1:])  27.1 us
  transfers between devices with their start and end apart: 13, of which 11 were waited for; matrix products, arithmetic and copies ran while one was open for 6% of the time, Pallas kernels for 0%

profile of v1, /device:TPU:2, one launch (start us, length us, event | category | flops | bytes accessed | tf_op | source)
XLA Modules:
  0.0 565.0 jit_solution(5718748929242099711)
XLA Ops:
  9.5 11.5 %all-to-all-start = ((bf16[32,192,12]{1,2,0:T(8,128)(2,1)}), bf16[32,192,12]{1,2,0:T(8,128)(2,1)S(1)}, u32[]{:S(2)}, u32[]{:S(2)}) async-start(bf16[32,192,12]{1,2,0:T(8,128)(2,1)} %broadcast_in_dim.10), calls=%async_computation | async-start | bytes 524288 | tf_op jit(solution)/shard_map/all_to_all | solution.py:27
  22.6 12.0 %all-to-all-done = bf16[32,192,12]{1,2,0:T(8,128)(2,1)S(1)} async-done(((bf16[32,192,12]{1,2,0:T(8,128)(2,1)}), bf16[32,192,12]{1,2,0:T(8,128)(2,1)S(1)}, u32[]{:S(2)}, u32[]{:S(2)}) %all-to-all-start) | async-done | bytes 147488 | tf_op jit(solution)/shard_map/all_to_all | solution.py:27
  35.8 5.0 all-to-all-start.1
  41.5 16.6 %all-to-all-done.1 = bf16[8,512,160]{1,2,0:T(8,128)(2,1)S(1)} async-done(((bf16[8,512,160]{1,2,0:T(8,128)(2,1)}), bf16[8,512,160]{1,2,0:T(8,128)(2,1)S(1)}, u32[]{:S(2)}, u32[]{:S(2)}) %all-to-all-start.1) | async-done | bytes 1310752 | tf_op jit(solution)/shard_map/all_to_all | solution.py:27
  59.4 4.8 all-to-all-start.2
  64.4 113.4 %all-gather.1 = bf16[32,12,352]{2,1,0:T(8,128)(2,1)S(1)} all-gather(bf16[1,12,352]{2,1,0:T(8,128)(2,1)S(1)} %maximum_bitcast_fusion.1), channel_id=1, replica_groups=mesh['role'=2,'dp_0'=4,'dp_1'=4,'mp_0'=4,'mp_1'=2] {'role','dp_0','dp_1'}, dimensions={0}, use_global_device_ids=true | all-gather | bytes 278784 | tf_op jit(solution)/shard_map/all_gather | solution.py:56
  184.9 4.7 all-gather.5.cloned.1.call-done
  189.6 8.5 %conditional.1 = (f32[512,1280]{1,0:T(8,128)}) conditional(s32[]{:T(128)} %convert_element_type.100, () %tuple.14, (bf16[512,8,160]{0,2,1:T(8,128)(2,1)S(1)}, bf16[32,40,640]{2,1,0:T(8,128)(2,1)}, bf16[640,1280]{0,1:T(8,128)(2,1)}) %tuple.39), branch_computations={%region_5.0_spmd, %region_6.9_spmd} | conditional | flops 1687224832 | bytes 12470280 | solution.py:164
  191.7 6.4 %fusion.12 = f32[512,1280]{1,0:T(8,128)} fusion(bf16[640,1280]{0,1:T(8,128)(2,1)} %get-tuple-element.26, bf16[512,1280]{0,1:T(8,128)(2,1)} %bitcast.39, bf16[1280,640]{1,0:T(8,128)(2,1)} %bitcast.1), kind=kOutput, calls=%fused_computation.15 | convolution fusion | flops 1680670720 | bytes 7208960 | tf_op jit(solution)/shard_map/cond/branch_1_fun/dot_general | solution.py:159
  202.7 3.5 all-to-all-start.4
  206.8 7.1 %all-to-all-done.4 = f32[16,1,1]{2,1,0:T(1,128)S(1)} async-done(((f32[16,1,1]{2,1,0:T(1,128)}), f32[16,1,1]{2,1,0:T(1,128)S(1)}, u32[]{:S(2)}, u32[]{:S(2)}) %all-to-all-start.4) | async-done | bytes 96 | tf_op jit(solution)/shard_map/all_to_all | solution.py:27
  215.2 34.8 %all-reduce.5.cloned.1.call-done = f32[1024,384]{1,0:T(8,128)} async-done(((f32[1024,384]{1,0:T(8,128)}), f32[1024,384]{1,0:T(8,128)}) %all-reduce.5.cloned.1.call-update) | async-done | bytes 1572880 | tf_op jit(solution)/shard_map/psum | solution.py:195
  252.4 35.9 %reduce-scatter.3.cloned.1.call-done = f32[512,160]{0,1:T(8,128)} async-done(((f32[512,1280]{0,1:T(8,128)}), f32[512,160]{0,1:T(8,128)}) %reduce-scatter.3.cloned.1.call-update) | async-done | bytes 327696 | tf_op jit(solution)/shard_map/reduce_scatter | solution.py:165
  290.0 7.1 %all-to-all-start.3 = ((f32[8,1,1024]{2,1,0:T(1,128)}), f32[8,1,1024]{2,1,0:T(1,128)S(1)}, u32[]{:S(2)}, u32[]{:S(2)}) async-start(f32[8,1,1024]{2,1,0:T(1,128)} %broadcast_in_dim.12), calls=%async_computation.4 | async-start | bytes 65536 | tf_op jit(solution)/shard_map/all_to_all | solution.py:27
  297.1 4.0 all-to-all-done.3
  302.2 7.8 %collective-permute-start = (bf16[512,160]{0,1:T(8,128)(2,1)S(1)}, bf16[512,160]{0,1:T(8,128)(2,1)S(1)}, u32[]{:S(2)}, u32[]{:S(2)}) collective-permute-start(bf16[512,160]{0,1:T(8,128)(2,1)S(1)} %multiply_convert_fusion.2), channel_id=1, source_target_pairs={{0,128},{1,129},{2,130},{3,131},{4,132},{5,133},{6,134},{7,135},{8... | collective-permute-start | bytes 491528 | tf_op jit(solution)/shard_map/ppermute | solution.py:50
  316.8 35.9 %reduce-scatter.5.cloned.1.call-done = f32[128,384]{1,0:T(8,128)} async-done(((f32[1024,384]{1,0:T(8,128)}), f32[128,384]{1,0:T(8,128)}) %reduce-scatter.5.cloned.1.call-update) | async-done | bytes 196624 | tf_op jit(solution)/shard_map/reduce_scatter | solution.py:71
  354.6 27.1 %all-gather.7.cloned.1.call-done = f32[1024,384]{1,0:T(8,128)} async-done(((f32[128,384]{1,0:T(8,128)}), f32[1024,384]{1,0:T(8,128)}) %all-gather.7.cloned.1.call-update) | async-done | bytes 1572880 | tf_op jit(solution)/shard_map/all_gather | solution.py:74
  390.2 10.0 %all-to-all-start.5 = ((f32[32,192,12]{1,2,0:T(8,128)}), f32[32,192,12]{1,2,0:T(8,128)S(1)}, u32[]{:S(2)}, u32[]{:S(2)}) async-start(f32[32,192,12]{1,2,0:T(8,128)} %bitcast.10), calls=%async_computation.7 | async-start | bytes 1048576 | tf_op jit(solution)/shard_map/all_to_all | solution.py:99
  402.1 16.2 %psum.43 = f32[]{:T(128)} all-reduce(f32[]{:T(128)S(6)} %mul.193), channel_id=1, replica_groups=mesh['role'=2,'dp_0'=4,'dp_1'=4,'mp_0'=4,'mp_1'=2] {'role'}, use_global_device_ids=true, to_apply=%region_14.0 | all-reduce | flops 1 | bytes 8 | tf_op jit(solution)/shard_map/psum | solution.py:61
  418.4 10.4 %psum.44 = f32[]{:T(128)} all-reduce(f32[]{:T(128)} %psum.43), channel_id=1, replica_groups=mesh['role'=2,'dp_0'=4,'dp_1'=4,'mp_0'=4,'mp_1'=2] {'dp_0'}, use_global_device_ids=true, to_apply=%region_15.0 | all-reduce | flops 1 | bytes 8 | tf_op jit(solution)/shard_map/psum | solution.py:61
  429.4 10.3 %psum.45 = f32[]{:T(128)} all-reduce(f32[]{:T(128)} %psum.44), channel_id=1, replica_groups=mesh['role'=2,'dp_0'=4,'dp_1'=4,'mp_0'=4,'mp_1'=2] {'dp_1'}, use_global_device_ids=true, to_apply=%region_16.0 | all-reduce | flops 1 | bytes 8 | tf_op jit(solution)/shard_map/psum | solution.py:61
  440.3 10.4 %psum.46 = f32[]{:T(128)} all-reduce(f32[]{:T(128)} %psum.45), channel_id=1, replica_groups=mesh['role'=2,'dp_0'=4,'dp_1'=4,'mp_0'=4,'mp_1'=2] {'mp_0'}, use_global_device_ids=true, to_apply=%region_17.0 | all-reduce | flops 1 | bytes 8 | tf_op jit(solution)/shard_map/psum | solution.py:61
  454.4 98.4 %all-reduce.7.cloned.1.call-done = bf16[1280,128]{1,0:T(8,128)(2,1)} async-done(((bf16[1280,128]{1,0:T(8,128)(2,1)}), bf16[1280,128]{1,0:T(8,128)(2,1)}) %all-reduce.7.cloned.1.call-update) | async-done | bytes 327696
  (110 shorter events, 50.7 us)
Async XLA Ops:
  8.0 13.7 %copy-start = (bf16[1568,160]{0,1:T(8,128)(2,1)S(1)}, bf16[1568,160]{0,1:T(8,128)(2,1)}, u32[]{:S(2)}) copy-start(bf16[1568,160]{0,1:T(8,128)(2,1)} %param.12) | copy-start | bytes 1505284
  9.5 25.1 %all-to-all-start = ((bf16[32,192,12]{1,2,0:T(8,128)(2,1)}), bf16[32,192,12]{1,2,0:T(8,128)(2,1)S(1)}, u32[]{:S(2)}, u32[]{:S(2)}) async-start(bf16[32,192,12]{1,2,0:T(8,128)(2,1)} %broadcast_in_dim.10), calls=%async_computation | async-start | bytes 524288 | tf_op jit(solution)/shard_map/all_to_all | solution.py:27
  22.6 13.2 %copy-start.10 = (bf16[512,160]{0,1:T(8,128)(2,1)}, bf16[512,160]{0,1:T(8,128)(2,1)S(1)}, u32[]{:S(2)}) copy-start(bf16[512,160]{0,1:T(8,128)(2,1)S(1)} %fusion.31) | copy-start | bytes 491524
  35.8 22.3 %copy-start.15 = (bf16[40,640]{1,0:T(8,128)(2,1)S(1)}, bf16[40,640]{1,0:T(8,128)(2,1)}, u32[]{:S(2)}) copy-start(bf16[40,640]{1,0:T(8,128)(2,1)} %param.14) | copy-start | bytes 153604
  35.8 22.2 %all-to-all-start.1 = ((bf16[8,512,160]{1,2,0:T(8,128)(2,1)}), bf16[8,512,160]{1,2,0:T(8,128)(2,1)S(1)}, u32[]{:S(2)}, u32[]{:S(2)}) async-start(bf16[8,512,160]{1,2,0:T(8,128)(2,1)} %broadcast_in_dim.11), calls=%async_computation.1 | async-start | bytes 2621440 | tf_op jit(solution)/shard_map/all_to_all | solution.py:27
  40.7 148.9 %all-gather.5.cloned.1.call-start = ((), (), s32[]{:S(2)}) async-start(), calls=%async_computation.9 | async-start | bytes 1689600 | tf_op jit(solution)/shard_map/all_gather | solution.py:152
  59.4 4.9 copy-start.16
  59.4 4.9 copy-start.17
  59.4 119.2 %copy-start.1 = (bf16[1024,384]{1,0:T(8,128)(2,1)S(1)}, bf16[1024,384]{1,0:T(8,128)(2,1)}, u32[]{:S(2)}) copy-start(bf16[1024,384]{1,0:T(8,128)(2,1)} %param.13) | copy-start | bytes 2359300
  59.4 125.5 %all-to-all-start.2 = ((bf16[32,40,640]{2,1,0:T(8,128)(2,1)}), bf16[32,40,640]{2,1,0:T(8,128)(2,1)}, u32[]{:S(2)}, u32[]{:S(2)}) async-start(bf16[32,40,640]{2,1,0:T(8,128)(2,1)} %stack.2), calls=%async_computation.2 | async-start | bytes 3276800 | tf_op jit(solution)/shard_map/all_to_all | solution.py:151
  64.2 185.8 %all-reduce.5.cloned.1.call-start = ((), (), s32[]{:S(2)}) async-start(), calls=%async_computation.8 | async-start | bytes 3145728 | tf_op jit(solution)/shard_map/psum | solution.py:195
  180.3 4.5 copy-start.4
  184.8 103.4 %reduce-scatter.3.cloned.1.call-start = ((), (), s32[]{:S(2)}) async-start(), calls=%async_computation.10 | async-start | bytes 2949120 | tf_op jit(solution)/shard_map/reduce_scatter | solution.py:165
  202.7 11.3 %all-to-all-start.4 = ((f32[16,1,1]{2,1,0:T(1,128)}), f32[16,1,1]{2,1,0:T(1,128)S(1)}, u32[]{:S(2)}, u32[]{:S(2)}) async-start(f32[16,1,1]{2,1,0:T(1,128)} %broadcast_in_dim.13), calls=%async_computation.5 | async-start | bytes 16384 | tf_op jit(solution)/shard_map/all_to_all | solution.py:27
  251.8 36.5 %copy-start.11 = (bf16[512,160]{0,1:T(8,128)(2,1)S(1)}, bf16[512,160]{0,1:T(8,128)(2,1)}, u32[]{:S(2)}) copy-start(bf16[512,160]{0,1:T(8,128)(2,1)} %copy-done.10) | copy-start | bytes 491524
  290.0 11.1 %all-to-all-start.3 = ((f32[8,1,1024]{2,1,0:T(1,128)}), f32[8,1,1024]{2,1,0:T(1,128)S(1)}, u32[]{:S(2)}, u32[]{:S(2)}) async-start(f32[8,1,1024]{2,1,0:T(1,128)} %broadcast_in_dim.12), calls=%async_computation.4 | async-start | bytes 65536 | tf_op jit(solution)/shard_map/all_to_all | solution.py:27
  297.1 55.7 %reduce-scatter.5.cloned.1.call-start = ((), (), s32[]{:S(2)}) async-start(), calls=%async_computation.11 | async-start | bytes 1769472 | tf_op jit(solution)/shard_map/reduce_scatter | solution.py:71
  302.2 11.2 %copy-start.9 = (bf16[384,352]{1,0:T(8,128)(2,1)S(1)}, bf16[384,352]{1,0:T(8,128)(2,1)}, u32[]{:S(2)}) copy-start(bf16[384,352]{1,0:T(8,128)(2,1)} %reshape.201) | copy-start | bytes 811012
  302.2 11.2 %collective-permute-start = (bf16[512,160]{0,1:T(8,128)(2,1)S(1)}, bf16[512,160]{0,1:T(8,128)(2,1)S(1)}, u32[]{:S(2)}, u32[]{:S(2)}) collective-permute-start(bf16[512,160]{0,1:T(8,128)(2,1)S(1)} %multiply_convert_fusion.2), channel_id=1, source_target_pairs={{0,128},{1,129},{2,130},{3,131},{4,132},{5,133},{6,134},{7,135},{8... | collective-permute-start | bytes 491528 | tf_op jit(solution)/shard_map/ppermute | solution.py:50
  310.3 4.5 copy-start.7
  316.6 65.2 %all-gather.7.cloned.1.call-start = ((), (), s32[]{:S(2)}) async-start(), calls=%async_computation.12 | async-start | bytes 1769472 | tf_op jit(solution)/shard_map/all_gather | solution.py:74
  390.2 38.6 %copy-start.18 = (u32[256]{0:T(256)S(1)}, u32[256]{0:T(256)}, u32[]{:S(2)}) copy-start(u32[256]{0:T(256)} %constant.79) | copy-start | bytes 3076
  390.2 165.5 %all-to-all-start.5 = ((f32[32,192,12]{1,2,0:T(8,128)}), f32[32,192,12]{1,2,0:T(8,128)S(1)}, u32[]{:S(2)}, u32[]{:S(2)}) async-start(f32[32,192,12]{1,2,0:T(8,128)} %bitcast.10), calls=%async_computation.7 | async-start | bytes 1048576 | tf_op jit(solution)/shard_map/all_to_all | solution.py:99
  400.2 152.7 %all-reduce.7.cloned.1.call-start = ((), (), s32[]{:S(2)}) async-start(), calls=%async_computation.13 | async-start | bytes 655360
  (8 other events, 11.4 us)
Sparse Core Ops, SparseCore 0:
  43.3 146.2 all-gather.4
  404.4 148.3 all-reduce.6
Sparse Core Ops, SparseCore 1:
  184.9 65.0 all-reduce.4
  252.4 35.8 reduce-scatter.2
  316.7 36.0 reduce-scatter.4
  354.6 27.1 all-gather.6
